TPU v7x, 32 devices: a whole 2x2x4 slice. The times are simulated.
32 devices in a mesh: seq: 16 (over z, y, x), head: 2 (over core).
Axes of the slice: x: 2, y: 2, z: 4, core: 2. Of those that a mesh axis runs over, the one named last changes fastest.
Arguments:
- queries: bfloat16 [4096, 3584], P('seq', 'head'), may hold values from -5 to 5
- keys: bfloat16 [4096, 3584], P('seq', 'head'), may hold values from -5 to 5
- values: bfloat16 [4096, 3584], P('seq', 'head'), may hold values from -6 to 6
- attn_grad: bfloat16 [4096, 3584], P('seq', 'head'), may hold values from -6 to 6
- doc_ids: int32 [4096], replicated, may hold values from 0 to 3, never falling along the last dimension, each value on 1 to 2048 neighbouring positions
- conv_input: bfloat16 [4096, 7168], P('seq', 'head'), may hold values from -6 to 6
- conv_weight: float32 [4, 7168], P(None, 'head'), may hold values from -3 to 3
- step_raw: float32 [4096, 112], P('seq', 'head'), may hold values from -4 to 4
- step_bias: float32 [112], P('head'), may hold values from -1.5 to 0
- rate_log: float32 [112], P('head'), may hold values from -13 to -1
- skip_gain: float32 [112], P('head'), may hold values from 0.5 to 1.5
- input_coeff: bfloat16 [4096, 128], P('seq'), may hold values from -0.625 to 0.625
- output_coeff: bfloat16 [4096, 128], P('seq'), may hold values from -0.625 to 0.625
- gate_input: bfloat16 [4096, 7168], P('seq', 'head'), may hold values from -6 to 6
- mix_grad: bfloat16 [4096, 7168], P('seq', 'head'), may hold values from -1.5 to 1.5
Outputs:
- grad_queries: bfloat16 [4096, 3584], P('seq', 'head')
- grad_keys: bfloat16 [4096, 3584], P('seq', 'head')
- grad_values: bfloat16 [4096, 3584], P('seq', 'head')
- grad_conv_input: bfloat16 [4096, 7168], P('seq', 'head')
- grad_gate: bfloat16 [4096, 7168], P('seq', 'head')
- grad_step: float32 [4096, 112], P('seq', 'head')
- grad_input_coeff: float32 [4096, 128], P('seq')
- grad_output_coeff: float32 [4096, 128], P('seq')
- grad_conv_weight: float32 [4, 7168], P(None, 'head')
- grad_step_bias: float32 [112], P('head')
- grad_rate_log: float32 [112], P('head')
- grad_skip: float32 [112], P('head')
Inputs may be any that keep to these rules, and one draw needn't show every extreme that they name: doc_ids never fall along the sequence.
All inputs are finite; a program needn't handle non-finite values.
Results may differ from a plain program's by a relative error of at most 0.012.
Values may be sent and summed in bfloat16 or wider, within the bound.
A program may use at most 192 MiB of HBM per device.

v0:
```python
import functools
import types

import jax
import jax.numpy as jnp
from jax import lax
from jax.experimental import pallas as pl
from jax.experimental.pallas import tpu as pltpu
from jax.sharding import PartitionSpec as P

HEAD_DIM = 224
WIDE = 256
WINDOW = 1024
SSM_HEADS = 112
STATE = 64
GROUPS = 2
KERNEL = 4
PAD = 8
EDGE = 16
LANES = 128

EXACT = lax.Precision.HIGHEST
F32 = jnp.float32
BF16 = jnp.bfloat16
NEG_FILL = -1e30
SCALE = HEAD_DIM ** (-0.5)
MESH = pl.DeviceIdType.MESH


def dot(a, b, ca, cb, precision=None):
    return lax.dot_general(
        a, b, (((ca,), (cb,)), ((), ())), preferred_element_type=F32, precision=precision
    )


def aligned(first, size):
    return pl.ds(pl.multiple_of(first, size), size)


def iota(shape, dim):
    return lax.broadcasted_iota(jnp.int32, shape, dim)


class Exchange:
    def __init__(self, make, offsets):
        self.make, self.offsets = make, offsets

    def start(self):
        for d in self.offsets:
            self.make(d).start()

    def wait_recv(self):
        for d in self.offsets:
            self.make(d).wait_recv()

    def wait_send(self):
        for d in self.offsets:
            self.make(d).wait_send()


def remote(src, dst, sems, where, **device):
    return pltpu.make_async_remote_copy(
        src_ref=src, dst_ref=dst, send_sem=sems[0].at[where], recv_sem=sems[1].at[where],
        device_id=device, device_id_type=MESH,
    )


def expand(values, index):
    return jnp.take_along_axis(values, index, axis=1, mode="promise_in_bounds")


def turned(value):
    return value.astype(F32).T


def kernel(z, *refs):
    r = types.SimpleNamespace(**dict(zip(z.names, refs)))
    R, C, H, Hs, G = z.rows, z.channels, z.heads, z.ssm_heads, z.group
    per, span, CW = z.per, z.group * z.rows, z.chunk * LANES
    index = lax.axis_index("seq")
    head = lax.axis_index("head")
    place = lax.rem(index, G)
    base = index - place
    plane = lax.div(index, G)
    part = lax.div(head * Hs, SSM_HEADS // GROUPS)
    others = range(1, G)
    has_next, has_prev = index + G < z.count, index >= G

    def to_place(d):
        return lax.rem(place + d, G)

    def from_place(d):
        return lax.rem(place + G - d, G)

    def ring(at):
        return lax.rem(at + z.count, z.count)

    def kv_out(hh, d):
        p = to_place(d)
        return remote(
            r.send.at[per * p + hh, pl.ds(0, 2)], r.kv.at[hh, :, aligned(span + place * R, R)],
            (r.kv_s, r.kv_r), (hh, d), seq=base + p,
        )

    def qd_out(hh, d):
        p = to_place(d)
        return remote(
            r.send.at[per * p + hh, pl.ds(2, 2)], r.qd.at[hh, :, aligned(place * R, R)],
            (r.qd_s, r.qd_r), (hh, d), seq=base + p,
        )

    def forward(hh, d):
        p = from_place(d)
        return remote(
            r.kv.at[hh, :, aligned(span + p * R, R)], r.kv.at[hh, :, aligned(p * R, R)],
            (r.fw_s, r.fw_r), (hh, d), seq=ring(index + G),
        )

    def backward(hh, b):
        return remote(
            r.bks.at[hh, :, aligned(b * R, R)], r.bkr.at[hh, :, aligned(b * R, R)],
            (r.bk_s, r.bk_r), (hh, b), seq=ring(index - G),
        )

    def dq_out(hh, d):
        p = to_place(d)
        return remote(
            r.dq.at[hh, aligned(p * R, R)], r.fin.at[per * place + hh, 0],
            (r.dq_s, r.dq_r), (hh, d), seq=base + p,
        )

    def dkv_out(hh, d):
        p = to_place(d)
        return remote(
            r.kvo.at[hh, :, aligned(p * R, R)], r.fin.at[per * place + hh, pl.ds(1, 2)],
            (r.do_s, r.do_r), (hh, d), seq=base + p,
        )

    def tail_out():
        return remote(
            r.conv.at[pl.ds(R - EDGE, EDGE)], r.tail, (r.one_s, r.one_r), 0, seq=ring(index + 1)
        )

    def spill_out():
        return remote(r.edge, r.spill, (r.one_s, r.one_r), 1, seq=ring(index - 1))

    def state_out(d):
        p = to_place(d)
        return remote(r.st_s.at[p], r.st_a.at[place], (r.st_ss, r.st_sr), d, seq=base + p)

    def decay_out(d):
        p = to_place(d)
        return remote(r.th_s.at[p], r.th_a.at[place], (r.th_ss, r.th_sr), d, seq=base + p)

    def up_out(k):
        return remote(r.agg.at[0], r.up.at[k], (r.up_s, r.up_r), k, seq=ring(index + k * G))

    def up_decay(k):
        return remote(r.aggt, r.upt.at[k], (r.ut_s, r.ut_r), k, seq=ring(index + k * G))

    def down_out(k):
        return remote(r.agg.at[1], r.dn.at[k], (r.dn_s, r.dn_r), k, seq=ring(index - k * G))

    def down_decay(k):
        return remote(r.aggt, r.dnt.at[k], (r.dt_s, r.dt_r), k, seq=ring(index - k * G))

    def enter_out(d):
        p = to_place(d)
        return remote(r.ent_s.at[p], r.ent.at[place], (r.en_s, r.en_r), d, seq=base + p)

    def sum_out(d):
        p = to_place(d)
        return remote(r.red_s.at[p], r.red_a.at[place], (r.ra_s, r.ra_r), d, seq=base + p)

    def plane_out(k):
        return remote(
            r.red_p, r.red_z.at[plane], (r.rz_s, r.rz_r), k, seq=ring(index + k * G)
        )

    def total_out(d):
        return remote(r.red_t, r.red_o.at[place], (r.ro_s, r.ro_r), d, seq=base + to_place(d))

    def coeff_out(d):
        return remote(
            r.co_s, r.co_a.at[head], (r.co_ss, r.co_sr), d, head=lax.rem(head + d, z.head_count)
        )

    head_others = range(1, z.head_count)
    planes = z.count // G
    reach = range(1, z.reach + 1)

    @pl.when(index + 1 < z.count)
    def _():
        tail_out().start()

    @pl.when(index == 0)
    def _():
        r.tail[...] = jnp.zeros_like(r.tail)

    def window(h, ref):
        first = h * HEAD_DIM // LANES * LANES
        last = -(-(h + 1) * HEAD_DIM // LANES) * LANES
        return first, last, h * HEAD_DIM - first

    def pack(ref, h, a):
        first, last, off = window(h, ref)
        value = ref[:, first:last].astype(F32)
        if off:
            value = pltpu.roll(value, last - first - off, 1)
        value = value[:, :WIDE]
        keep = iota((R, WIDE), 1) < HEAD_DIM
        r.send[h, a] = jnp.where(keep, value, 0.0).astype(BF16)

    def own_piece(hh):
        mine = per * place + hh
        for a in range(2):
            r.kv[hh, a, aligned(span + place * R, R), :] = r.send[mine, a]
            r.qd[hh, a, aligned(place * R, R), :] = r.send[mine, 2 + a]

    for h in range(H):
        for a, ref in enumerate((r.k, r.v, r.q, r.do)):
            pack(ref, h, a)
    for hh in range(per):
        for d in others:
            kv_out(hh, d).start()
        for d in others:
            qd_out(hh, d).start()
    for hh in range(per):
        own_piece(hh)

    @pl.when(has_next)
    def _():
        for hh in range(per):
            forward(hh, 0).start()

    @pl.when(jnp.logical_not(has_prev))
    def _():
        for hh in range(per):
            for a in range(2):
                r.kv[hh, a, pl.ds(0, span), :] = jnp.zeros((span, WIDE), BF16)

    @pl.when(jnp.logical_not(has_next))
    def _():
        r.bkr[...] = jnp.zeros_like(r.bkr)

    def pass_on(hh, d):
        kv_out(hh, d).wait_recv()

        @pl.when(has_next)
        def _():
            forward(hh, d).start()

    for t in range(2 * G):
        row = r.docs[pl.ds(base + t, 1), :]
        r.dcol[t * R : (t + 1) * R, :] = jnp.broadcast_to(row, (LANES, R)).T
    own_doc = span + place * R
    r.mext[...] = r.dcol[pl.ds(pl.multiple_of(own_doc - PAD, PAD), R + PAD), :]
    doc_now = r.mext[PAD:, :]
    for lag in range(1, KERNEL):
        r.mask[lag - 1] = (r.mext[PAD - lag : PAD - lag + R, :] == doc_now).astype(F32)
    i2, j2 = iota((R, R), 0), iota((R, R), 1)
    doc_row = r.docs[pl.ds(index + G, 1), :]
    doc_pair = jnp.concatenate([doc_now] * (R // LANES), axis=1)
    r.bias[...] = jnp.where((i2 >= j2) & (doc_pair == doc_row), 0.0, NEG_FILL)

    r.raw[...] = jnp.zeros_like(r.raw)
    r.raw[:, :Hs] = r.step_raw[...] + r.step_bias[...]
    r.head_rows[...] = jnp.zeros_like(r.head_rows)
    r.head_rows[0:1, :Hs] = jnp.exp(r.rate_log[...])
    r.head_rows[1:2, :Hs] = r.skip_gain[...]
    raw = r.raw[...]
    rate = r.head_rows[0:1, :]
    size_all = jnp.maximum(raw, 0.0) + jnp.log1p(jnp.exp(-jnp.abs(raw)))
    log_decay = -size_all * rate
    tri = (i2 >= j2).astype(F32)
    cum = dot(tri, log_decay, 1, 0, EXACT)
    enter_all = jnp.where(doc_now == r.mext[PAD - 1 : PAD, :], jnp.exp(cum), 0.0)
    to_end_all = jnp.where(
        doc_now == r.mext[R + PAD - 1 : R + PAD, :], jnp.exp(cum[R - 1 : R, :] - cum), 0.0
    )
    r.cum[...] = cum
    r.cumt[...] = cum.T
    r.size[...] = size_all
    r.enter[...] = enter_all
    r.to_end[...] = to_end_all

    b_wide, c_wide = r.b_in[...], r.c_in[...]
    b_own, c_own = b_wide[:, :STATE], c_wide[:, :STATE]
    for g in range(1, GROUPS):
        b_own = jnp.where(part == g, b_wide[:, g * STATE : (g + 1) * STATE], b_own)
        c_own = jnp.where(part == g, c_wide[:, g * STATE : (g + 1) * STATE], c_own)
    r.b[...] = b_own
    r.c[...] = c_own
    r.bt[...] = turned(b_own).astype(BF16)
    r.ct[...] = turned(c_own).astype(BF16)
    r.pair[...] = dot(c_own, b_own, 1, 1)

    @pl.when(index > 0)
    def _():
        tail_out().wait_recv()

    lower = iota((R, LANES), 1) < LANES // 2
    half = jnp.where(lower, 0, 1)

    def conv_pre(lanes):
        r.xp[:PAD, :] = r.tail[:, lanes].astype(F32)[EDGE - PAD :, :]
        r.xp[PAD:, :] = r.conv[:, lanes].astype(F32)
        pre = r.cw[0:1, lanes] * r.xp[PAD:, :]
        for lag in range(1, KERNEL):
            pre = pre + r.cw[lag : lag + 1, lanes] * (
                r.xp[PAD - lag : PAD - lag + R, :] * r.mask[lag - 1]
            )
        return pre

    def ends(c):
        def one(m, carry):
            p = c * z.chunk + m
            lanes = aligned(p * LANES, LANES)
            here = aligned(m * LANES, LANES)
            pre = conv_pre(lanes)
            act = pre * jax.nn.sigmoid(pre)
            who = half + 2 * p
            enter = expand(r.enter[...], who)
            weighted = act * expand(r.size[...], who) * expand(r.to_end[...], who)
            r.st_s[c, 0, :, here] = dot(r.bt[...], weighted.astype(BF16), 1, 0).astype(BF16)
            gate = r.gate[:, lanes].astype(F32)
            dy = r.mix[:, lanes].astype(F32) * (gate * jax.nn.sigmoid(gate))
            r.st_s[c, 1, :, here] = dot(r.ct[...], (dy * enter).astype(BF16), 1, 0).astype(BF16)
            r.th_s[c, :, here] = jnp.broadcast_to(enter[R - 1 : R, :], (PAD, LANES))
            return carry

        lax.fori_loop(0, z.chunks[c], one, 0)

    if z.padded:
        r.st_s[...] = jnp.zeros_like(r.st_s)
        r.th_s[...] = jnp.zeros_like(r.th_s)
        r.red_s[...] = jnp.zeros_like(r.red_s)

    for c in range(G):
        ends(c)
        if c > 0:
            pass_on(0, c)
    state, decay = Exchange(state_out, others), Exchange(decay_out, others)
    state.start()
    decay.start()
    r.st_a[place] = r.st_s[place]
    r.th_a[place] = r.th_s[place]

    r.dkv[...] = jnp.zeros_like(r.dkv)

    def attention(hh):
        j, i = iota((R, R), 0), iota((R, R), 1)

        def block(b, carry):
            mine = aligned(b * R, R)
            q = r.qd[hh, 0, mine, :]
            grad = r.qd[hh, 1, mine, :]
            docq = r.docs[pl.ds(base + G + b, 1), :]
            places = [aligned((b + G - gap) * R, R) for gap in range(G + 1)]
            scores = []
            top = None
            for gap in range(G + 1):
                dock = r.dcol[places[gap], :]
                allowed = jnp.concatenate([dock] * (R // LANES), axis=1) == docq
                if gap == 0:
                    allowed = allowed & (i >= j)
                if gap == G:
                    allowed = allowed & (i < j)
                s = jnp.where(allowed, dot(r.kv[hh, 0, places[gap], :], q, 1, 1) * SCALE, NEG_FILL)
                scores.append(s)
                m = jnp.max(s, axis=0, keepdims=True)
                top = m if top is None else jnp.maximum(top, m)
            total = None
            expo = []
            for gap in range(G + 1):
                e = jnp.exp(scores[gap] - top)
                expo.append(e)
                t = jnp.sum(e, axis=0, keepdims=True)
                total = t if total is None else total + t
            inverse = 1.0 / jnp.maximum(total, 1.0)
            delta = None
            dprobs = []
            for gap in range(G + 1):
                weight = (expo[gap] * inverse).astype(BF16)
                dp = dot(r.kv[hh, 1, places[gap], :], grad, 1, 1)
                d = jnp.sum(weight.astype(F32) * dp, axis=0, keepdims=True)
                delta = d if delta is None else delta + d
                r.dkv[hh, 1, places[gap], :] += dot(weight, grad, 1, 0)
                dprobs.append(dp)
            dq = None
            for gap in range(G + 1):
                ds = (expo[gap] * inverse * (dprobs[gap] - delta)).astype(BF16)
                r.dkv[hh, 0, places[gap], :] += dot(ds, q, 1, 0)
                piece = dot(ds, r.kv[hh, 0, places[gap], :], 0, 0)
                dq = piece if dq is None else dq + piece
            r.dq[hh, mine, :] = (dq * SCALE).astype(BF16)

            @pl.when(has_prev)
            def _():
                for a in range(2):
                    r.bks[hh, a, mine, :] = r.dkv[hh, a, mine, :].astype(BF16)
                backward(hh, b).start()

            return carry

        lax.fori_loop(0, G, block, 0)
        for d in others:
            dq_out(hh, d).start()
        r.fin[per * place + hh, 0] = r.dq[hh, aligned(place * R, R), :]

    def attention_inputs(hh):
        for d in others:
            qd_out(hh, d).wait_recv()

        @pl.when(has_prev)
        def _():
            for d in range(G):
                forward(hh, d).wait_recv()

    def give_back(hh):
        @pl.when(has_next)
        def _():
            for b in range(G):
                backward(hh, b).wait_recv()

        for t in range(G):
            rows = slice(t * R, (t + 1) * R)
            own = slice(span + t * R, span + (t + 1) * R)
            dk = (r.dkv[hh, 0, own, :] + r.bkr[hh, 0, rows, :].astype(F32)) * SCALE
            dv = r.dkv[hh, 1, own, :] + r.bkr[hh, 1, rows, :].astype(F32)
            r.kvo[hh, 0, rows, :] = dk.astype(BF16)
            r.kvo[hh, 1, rows, :] = dv.astype(BF16)
        for d in others:
            dkv_out(hh, d).start()
        for a in range(2):
            r.fin[per * place + hh, 1 + a] = r.kvo[hh, a, aligned(place * R, R), :]

    def tall(rows):
        return jnp.concatenate([rows] * (STATE // PAD), axis=0)

    def through(t, here):
        return tall(r.th_a[t, :, here])

    def chain_out():
        state.wait_recv()
        decay.wait_recv()
        def one(m, carry):
            here = aligned(m * LANES, LANES)
            a = r.st_a[0, 0, :, here].astype(F32)
            thr = r.th_a[0, :, here]
            for t in range(1, G):
                a = a * through(t, here) + r.st_a[t, 0, :, here].astype(F32)
                thr = thr * r.th_a[t, :, here]
            b = r.st_a[G - 1, 1, :, here].astype(F32)
            for t in range(G - 2, -1, -1):
                b = b * through(t, here) + r.st_a[t, 1, :, here].astype(F32)
            r.agg[0, :, here] = a.astype(BF16)
            r.agg[1, :, here] = b.astype(BF16)
            r.aggt[:, here] = thr
            return carry

        lax.fori_loop(0, z.chunk, one, 0)
        for k in reach:
            @pl.when(index + k * G < z.count)
            def _():
                up_out(k).start()
                up_decay(k).start()

            @pl.when(index + k * G >= z.count)
            def _():
                r.dn[k] = jnp.zeros((STATE, CW), BF16)
                r.dnt[k] = jnp.zeros((PAD, CW), F32)

            @pl.when(index - k * G >= 0)
            def _():
                down_out(k).start()
                down_decay(k).start()

            @pl.when(index - k * G < 0)
            def _():
                r.up[k] = jnp.zeros((STATE, CW), BF16)
                r.upt[k] = jnp.zeros((PAD, CW), F32)

    def chain_in():
        for k in reach:
            @pl.when(index - k * G >= 0)
            def _():
                up_out(k).wait_recv()
                up_decay(k).wait_recv()

            @pl.when(index + k * G < z.count)
            def _():
                down_out(k).wait_recv()
                down_decay(k).wait_recv()

        def one(m, carry):
            here = aligned(m * LANES, LANES)
            s = jnp.zeros((STATE, LANES), F32)
            e = jnp.zeros((STATE, LANES), F32)
            for k in reversed(reach):
                s = s * tall(r.upt[k, :, here]) + r.up[k, :, here].astype(F32)
                e = e * tall(r.dnt[k, :, here]) + r.dn[k, :, here].astype(F32)
            for t in range(G):
                r.ent_s[t, 0, :, here] = s.astype(BF16)
                s = s * through(t, here) + r.st_a[t, 0, :, here].astype(F32)
            for t in range(G - 1, -1, -1):
                r.ent_s[t, 1, :, here] = e.astype(BF16)
                e = e * through(t, here) + r.st_a[t, 1, :, here].astype(F32)
            return carry

        lax.fori_loop(0, z.chunk, one, 0)
        for d in others:
            enter_out(d).start()
        r.ent[place] = r.ent_s[place]

    r.dpair[...] = jnp.zeros_like(r.dpair)
    r.db[...] = jnp.zeros_like(r.db)
    r.dc[...] = jnp.zeros_like(r.dc)
    r.zsum[...] = jnp.zeros_like(r.zsum)
    r.usum[...] = jnp.zeros_like(r.usum)
    r.acc[...] = jnp.zeros_like(r.acc)
    r.dpad[...] = jnp.zeros_like(r.dpad)
    lane = iota((R, LANES), 1)
    lane_row = iota((PAD, LANES), 1)

    def mixer(c):
        def one(m, carry):
            p = c * z.chunk + m
            lanes = aligned(p * LANES, LANES)
            here = aligned(m * LANES, LANES)
            who = half + 2 * p
            size = expand(r.size[...], who)
            enter = expand(r.enter[...], who)
            to_end = expand(r.to_end[...], who)
            pre = conv_pre(lanes)
            sig_pre = jax.nn.sigmoid(pre)
            act = pre * sig_pre
            x_half = (act * size).astype(BF16)
            gate = r.gate[:, lanes].astype(F32)
            sig_gate = jax.nn.sigmoid(gate)
            silu_gate = gate * sig_gate
            cot = r.mix[:, lanes].astype(F32)
            dy = cot * silu_gate
            dy_half = dy.astype(BF16)
            state_in = r.ent[c, 0, :, here]
            end_cot = r.ent[c, 1, :, here]
            zero = jnp.zeros_like(dy_half)
            y_parts, dx_parts = [], []
            dpair = r.dpair[...]
            for k in range(2):
                column = expand(r.cum[...], jnp.zeros((R, LANES), jnp.int32) + (2 * p + k))
                column = jnp.concatenate([column] * (R // LANES), axis=1)
                weights = jnp.exp((column - r.cumt[pl.ds(2 * p + k, 1), :]) + r.bias[...])
                mixing = (r.pair[...] * weights).astype(BF16)
                y_parts.append(dot(mixing, x_half, 1, 0))
                dx_parts.append(dot(mixing, dy_half, 0, 0))
                dy_one = jnp.where(lower if k == 0 else ~lower, dy_half, zero)
                dpair = dpair + dot(dy_one, x_half, 1, 1) * weights
            r.dpair[...] = dpair
            inner = jnp.where(lower, y_parts[0], y_parts[1]) + enter * dot(r.c[...], state_in, 1, 0)
            end_part = to_end * dot(r.b[...], end_cot, 1, 0)
            dx = jnp.where(lower, dx_parts[0], dx_parts[1]) + end_part
            skip = expand(jnp.broadcast_to(r.head_rows[1:2, :], (PAD, LANES)), who[:PAD])[0:1]
            y = inner + skip * act
            r.ggate[:, lanes] = (cot * y * (sig_gate + silu_gate * (1.0 - sig_gate))).astype(BF16)
            x_wide = x_half.astype(F32)
            zed = dy_half.astype(F32) * inner - x_wide * dx
            you = dx * act
            r.dc[...] += dot((enter * dy).astype(BF16), state_in, 1, 1)
            r.db[...] += dot((to_end * x_wide).astype(BF16), end_cot, 1, 1)
            dact = dx * size + skip * dy
            dpre = dact * (sig_pre + act * (1.0 - sig_pre))
            sums = [jnp.sum(dpre * r.xp[PAD:, :], axis=0, keepdims=True)]
            r.dpad[0, PAD : PAD + R, :] = dpre
            grown = r.cw[0:1, lanes] * r.dpad[0, 0 : R + PAD, :]
            for lag in range(1, KERNEL):
                masked = dpre * r.mask[lag - 1]
                sums.append(
                    jnp.sum(masked * r.xp[PAD - lag : PAD - lag + R, :], axis=0, keepdims=True)
                )
                r.dpad[lag, PAD : PAD + R, :] = masked
                grown = grown + r.cw[lag : lag + 1, lanes] * r.dpad[lag, lag : lag + R + PAD, :]
            r.gconv[:, lanes] = grown[PAD:, :].astype(BF16)
            r.edge[:, lanes] = grown[:PAD, :]
            r.keep[:, lanes] = grown[R + PAD - EDGE :, :]
            none = jnp.zeros((PAD - KERNEL, LANES), F32)
            r.red_s[c, :, here] = jnp.concatenate(sums + [none], axis=0)
            heads3 = jnp.concatenate(
                [
                    jnp.sum(dy * act, axis=0, keepdims=True),
                    jnp.sum(state_in.astype(F32) * end_cot.astype(F32), axis=0, keepdims=True),
                    jnp.sum(x_wide * end_part, axis=0, keepdims=True),
                    jnp.zeros((PAD - 3, LANES), F32),
                ],
                axis=0,
            )
            for k in range(2):
                side = lower if k == 0 else ~lower
                mine = lane == 2 * p + k
                z_one = jnp.sum(jnp.where(side, zed, 0.0), axis=1, keepdims=True)
                u_one = jnp.sum(jnp.where(side, you, 0.0), axis=1, keepdims=True)
                h_one = jnp.sum(jnp.where(side[:PAD], heads3, 0.0), axis=1, keepdims=True)
                r.zsum[...] = jnp.where(mine, z_one, r.zsum[...])
                r.usum[...] = jnp.where(mine, u_one, r.usum[...])
                r.acc[...] = jnp.where(lane_row == 2 * p + k, h_one, r.acc[...])
            return carry

        lax.fori_loop(0, z.chunks[c], one, 0)

    def mixer_start():
        for d in others:
            enter_out(d).wait_recv()

    def mixer_end():
        @pl.when(index > 0)
        def _():
            spill_out().start()

        total = r.dpair[...]
        dc = r.dc[...] + dot(total, r.b[...].astype(F32), 1, 0, EXACT)
        db = r.db[...] + dot(total, r.c[...].astype(F32), 0, 0, EXACT)
        mine = lax.div(lane, STATE) == part
        r.co_s[0] = jnp.where(mine, jnp.concatenate([db] * GROUPS, axis=1), 0.0)
        r.co_s[1] = jnp.where(mine, jnp.concatenate([dc] * GROUPS, axis=1), 0.0)
        for d in head_others:
            coeff_out(d).start()
        r.co_a[head] = r.co_s[...]
        last_row = r.acc[2:3, :] + r.enter[R - 1 : R, :] * r.acc[1:2, :]
        rows = iota((R, LANES), 0)
        dcum = r.zsum[...] + jnp.where(rows == R - 1, last_row, 0.0)
        upper = (iota((R, R), 0) <= iota((R, R), 1)).astype(F32)
        dlog = dot(upper, dcum, 1, 0, EXACT)
        rates = r.head_rows[0:1, :]
        grad_step = (r.usum[...] - dlog * rates) * jax.nn.sigmoid(r.raw[...])
        r.gstep[...] = grad_step[:, :Hs]
        small = jnp.concatenate(
            [
                jnp.zeros((KERNEL, LANES), F32),
                jnp.sum(grad_step, axis=0, keepdims=True),
                jnp.sum(dlog * (-r.size[...] * rates), axis=0, keepdims=True),
                r.acc[0:1, :],
                jnp.zeros((1, LANES), F32),
            ],
            axis=0,
        )
        r.red_s[0, :, 0:LANES] += small
        for d in others:
            sum_out(d).start()
        r.red_a[place] = r.red_s[place]

    def sums_planes():
        for d in others:
            sum_out(d).wait_recv()
        total = r.red_a[0]
        for t in range(1, G):
            total = total + r.red_a[t]
        r.red_p[...] = total
        for k in range(1, planes):
            plane_out(k).start()
        r.red_z[plane] = total

    def sums_all():
        for k in range(1, planes):
            plane_out(k).wait_recv()
        total = r.red_z[0]
        for t in range(1, planes):
            total = total + r.red_z[t]
        r.red_t[...] = total
        for d in others:
            total_out(d).start()
        r.red_o[place] = total

    def sums_end():
        for d in others:
            total_out(d).wait_recv()
        for c in range(G):
            width = z.chunks[c] * LANES
            if width:
                r.gcw[:, c * CW : c * CW + width] = r.red_o[c, 0:KERNEL, 0:width]
        r.small[...] = r.red_o[0, :, 0:LANES]
        for d in head_others:
            coeff_out(d).wait_recv()
        db, dc = r.co_a[0, 0], r.co_a[0, 1]
        for d in head_others:
            db = db + r.co_a[d, 0]
            dc = dc + r.co_a[d, 1]
        r.gb[...] = db
        r.gc[...] = dc

        @pl.when(index + 1 < z.count)
        def _():
            spill_out().wait_recv()

        @pl.when(index + 1 >= z.count)
        def _():
            r.spill[...] = jnp.zeros_like(r.spill)

        spill = jnp.concatenate([jnp.zeros((EDGE - PAD, C), F32), r.spill[...]], axis=0)
        r.gconv[R - EDGE :, :] = (r.keep[...] + spill).astype(BF16)

    def unpack():
        for hh in range(per):
            for d in others:
                dq_out(hh, d).wait_recv()
                dkv_out(hh, d).wait_recv()
        for a, ref in enumerate((r.gq, r.gk, r.gv)):
            open_tile = None
            for h in range(H):
                first, last, off = window(h, ref)
                value = r.fin[h, a].astype(F32)
                if last - first > WIDE:
                    value = jnp.concatenate([value, jnp.zeros((R, LANES), F32)], axis=1)
                if off:
                    value = pltpu.roll(value, off, 1)
                tiles = [value[:, n : n + LANES] for n in range(0, last - first, LANES)]
                if off:
                    tiles[0] = tiles[0] + open_tile
                done = (h + 1) * HEAD_DIM % LANES == 0
                for n, tile in enumerate(tiles if done else tiles[:-1]):
                    ref[:, first + n * LANES : first + (n + 1) * LANES] = tile.astype(BF16)
                open_tile = tiles[-1]

    for hh in range(1, per):
        for d in others:
            pass_on(hh, d)
    attention_inputs(0)
    attention(0)
    chain_out()
    for hh in range(1, per):
        attention_inputs(hh)
        attention(hh)
    chain_in()
    mixer_start()
    for c in range(G):
        mixer(c)
        if c < per:
            give_back(c)
    for hh in range(G, per):
        give_back(hh)
    mixer_end()
    sums_planes()
    unpack()
    sums_all()
    sums_end()

    for hh in range(per):
        for d in others:
            kv_out(hh, d).wait_send()
            qd_out(hh, d).wait_send()
            dq_out(hh, d).wait_send()
            dkv_out(hh, d).wait_send()

    @pl.when(has_next)
    def _():
        for hh in range(per):
            for d in range(G):
                forward(hh, d).wait_send()

    @pl.when(has_prev)
    def _():
        for hh in range(per):
            for b in range(G):
                backward(hh, b).wait_send()

    state.wait_send()
    decay.wait_send()
    for d in others:
        enter_out(d).wait_send()
        sum_out(d).wait_send()
        total_out(d).wait_send()
    for k in range(1, planes):
        plane_out(k).wait_send()
    for d in head_others:
        coeff_out(d).wait_send()
    for k in reach:
        @pl.when(index + k * G < z.count)
        def _():
            up_out(k).wait_send()
            up_decay(k).wait_send()

        @pl.when(index - k * G >= 0)
        def _():
            down_out(k).wait_send()
            down_decay(k).wait_send()

    @pl.when(index + 1 < z.count)
    def _():
        tail_out().wait_send()

    @pl.when(index > 0)
    def _():
        spill_out().wait_send()


def local(
    queries, keys, values, attn_grad, doc_ids, conv_input, conv_weight, step_raw, step_bias,
    rate_log, skip_gain, input_coeff, output_coeff, gate_input, mix_grad,
):
    rows, width = queries.shape
    channels = conv_input.shape[1]
    ssm_heads = step_raw.shape[1]
    heads = width // HEAD_DIM
    count, head_count = lax.axis_size("seq"), lax.axis_size("head")
    group = WINDOW // rows
    pairs = channels // LANES
    chunk = -(-pairs // group)
    chunks = [max(0, min(chunk, pairs - c * chunk)) for c in range(group)]
    per = heads // group
    span, cw, planes = group * rows, chunk * LANES, count // group
    reach = max(1, min(planes - 1, -(-(count // 2) // group)))
    docs = jnp.pad(doc_ids.astype(F32), (span, 0), constant_values=-1.0).reshape(count + group, rows)

    vm, dma = pltpu.VMEM, pltpu.SemaphoreType.DMA
    inputs = dict(
        q=queries, k=keys, v=values, do=attn_grad, docs=docs, conv=conv_input, gate=gate_input,
        mix=mix_grad, cw=conv_weight, step_raw=step_raw, step_bias=step_bias[None],
        rate_log=rate_log[None], skip_gain=skip_gain[None], b_in=input_coeff, c_in=output_coeff,
    )
    outputs = dict(
        gq=((rows, width), BF16), gk=((rows, width), BF16), gv=((rows, width), BF16),
        gconv=((rows, channels), BF16), ggate=((rows, channels), BF16),
        gstep=((rows, ssm_heads), F32), gb=((rows, LANES), F32), gc=((rows, LANES), F32),
        gcw=((KERNEL, channels), F32), small=((PAD, LANES), F32),
    )
    scratch = dict(
        send=vm((heads, 4, rows, WIDE), BF16),
        kv=vm((per, 2, 2 * span, WIDE), BF16),
        qd=vm((per, 2, span, WIDE), BF16),
        dq=vm((per, span, WIDE), BF16),
        dkv=vm((per, 2, 2 * span, WIDE), F32),
        bks=vm((per, 2, span, WIDE), BF16),
        bkr=vm((per, 2, span, WIDE), BF16),
        kvo=vm((per, 2, span, WIDE), BF16),
        fin=vm((heads, 3, rows, WIDE), BF16),
        dcol=vm((2 * span, LANES), F32),
        mext=vm((rows + PAD, LANES), F32),
        mask=vm((KERNEL - 1, rows, LANES), F32),
        bias=vm((rows, rows), F32), pair=vm((rows, rows), F32), dpair=vm((rows, rows), F32),
        raw=vm((rows, LANES), F32), head_rows=vm((PAD, LANES), F32),
        cum=vm((rows, LANES), F32), cumt=vm((LANES, rows), F32), size=vm((rows, LANES), F32),
        enter=vm((rows, LANES), F32), to_end=vm((rows, LANES), F32),
        zsum=vm((rows, LANES), F32), usum=vm((rows, LANES), F32), acc=vm((PAD, LANES), F32),
        b=vm((rows, STATE), BF16), c=vm((rows, STATE), BF16),
        bt=vm((STATE, rows), BF16), ct=vm((STATE, rows), BF16),
        db=vm((rows, STATE), F32), dc=vm((rows, STATE), F32),
        xp=vm((rows + PAD, LANES), F32), dpad=vm((KERNEL, rows + 2 * PAD, LANES), F32),
        tail=vm((EDGE, channels), BF16), edge=vm((PAD, channels), F32),
        spill=vm((PAD, channels), F32), keep=vm((EDGE, channels), F32),
        st_s=vm((group, 2, STATE, cw), BF16), st_a=vm((group, 2, STATE, cw), BF16),
        th_s=vm((group, PAD, cw), F32), th_a=vm((group, PAD, cw), F32),
        agg=vm((2, STATE, cw), BF16), aggt=vm((PAD, cw), F32),
        up=vm((reach + 1, STATE, cw), BF16), dn=vm((reach + 1, STATE, cw), BF16),
        upt=vm((reach + 1, PAD, cw), F32), dnt=vm((reach + 1, PAD, cw), F32),
        ent_s=vm((group, 2, STATE, cw), BF16), ent=vm((group, 2, STATE, cw), BF16),
        red_s=vm((group, PAD, cw), F32), red_a=vm((group, PAD, cw), F32),
        red_p=vm((PAD, cw), F32), red_z=vm((planes, PAD, cw), F32),
        red_t=vm((PAD, cw), F32), red_o=vm((group, PAD, cw), F32),
        co_s=vm((2, rows, LANES), F32), co_a=vm((head_count, 2, rows, LANES), F32),
        one_s=dma((2,)), one_r=dma((2,)),
    )
    for name in ("kv", "qd", "fw", "bk", "dq", "do"):
        scratch[f"{name}_s"], scratch[f"{name}_r"] = dma((per, group)), dma((per, group))
    for name, size in (("st_s", group), ("th_s", group), ("co_s", head_count)):
        scratch[f"{name}s"], scratch[f"{name}r"] = dma((size,)), dma((size,))
    for name in ("up", "ut", "dn", "dt"):
        scratch[f"{name}_s"], scratch[f"{name}_r"] = dma((reach + 1,)), dma((reach + 1,))
    for name in ("en", "ra", "ro"):
        scratch[f"{name}_s"], scratch[f"{name}_r"] = dma((group,)), dma((group,))
    scratch["rz_s"], scratch["rz_r"] = dma((planes,)), dma((planes,))

    sizes = types.SimpleNamespace(
        rows=rows, channels=channels, heads=heads, ssm_heads=ssm_heads, group=group, per=per,
        chunk=chunk, chunks=chunks, padded=pairs % group != 0, count=count, reach=reach,
        head_count=head_count, names=[*inputs, *outputs, *scratch],
    )
    vmem = pl.BlockSpec(memory_space=pltpu.VMEM)
    gq, gk, gv, gconv, ggate, gstep, gb, gc, gcw, small = pl.pallas_call(
        functools.partial(kernel, sizes),
        in_specs=[vmem] * len(inputs),
        out_specs=[vmem] * len(outputs),
        out_shape=[jax.ShapeDtypeStruct(*o) for o in outputs.values()],
        scratch_shapes=list(scratch.values()),
        name="pair",
        compiler_params=pltpu.CompilerParams(
            vmem_limit_bytes=67_043_328, has_side_effects=True
        ),
        cost_estimate=pl.CostEstimate(
            flops=60_000_000_000, bytes_accessed=20_000_000, transcendentals=0
        ),
    )(*inputs.values())
    bias, rate, skip = (small[KERNEL + n, :ssm_heads] for n in range(3))
    return gq, gk, gv, gconv, ggate, gstep, gb, gc, gcw, bias, rate, skip


def solution(mesh):
    sharded = P("seq", "head")
    return jax.shard_map(
        local,
        mesh=mesh,
        in_specs=(
            sharded, sharded, sharded, sharded, P(), sharded, P(None, "head"), sharded,
            P("head"), P("head"), P("head"), P("seq", None), P("seq", None), sharded, sharded,
        ),
        out_specs=(
            sharded, sharded, sharded, sharded, sharded, sharded,
            P("seq", None), P("seq", None), P(None, "head"), P("head"), P("head"), P("head"),
        ),
        check_vma=False,
    )
```

profile of v0, /device:TPU:0, one launch (start us, length us, event | category | flops | bytes accessed | tf_op | source)
XLA Modules:
  0.0 162.7 jit_solution(14097805908280391270)
XLA Ops:
  0.6 0.7 convert_element_type.3
  1.4 0.6 reshape.27.refs_4_
  2.0 1.6 copy.27.refs_9_
  3.6 146.7 %pair.1 = (bf16[256,1792]{1,0:T(8,128)(2,1)}, bf16[256,1792]{1,0:T(8,128)(2,1)}, bf16[256,1792]{1,0:T(8,128)(2,1)}, bf16[256,3584]{1,0:T(8,128)(2,1)}, bf16[256,...) custom-call(bf16[256,1792]{1,0:T(8,128)(2,1)} %refs_0_.1, ...), custom_call_target="tpu_custom_call" | custom-call | flops 60000002048 | bytes 20000000 | tf_op jit(solution)/shard_map/pair/pallas_call | solution.py:877
  150.3 0.0 copy-start.3
  150.3 1.3 slice_bitcast_fusion
  151.6 1.6 copy.28
  153.2 0.0 copy-start.2
  153.2 2.2 %copy.37 = bf16[256,1792]{1,0:T(8,128)(2,1)} copy(bf16[256,1792]{1,0:T(8,128)(2,1)} %get-tuple-element.59) | data formatting | bytes 1835008
  155.5 0.0 copy-done.3
  155.5 0.0 copy-start.1
  155.5 0.9 copy.38
  156.4 0.0 copy-done.2
  156.4 0.9 copy.39
  157.3 0.0 copy-done.1
  157.3 0.0 copy-start
  157.3 1.2 copy.40
  158.6 0.9 copy-done
  159.5 0.0 copy-start.5
  159.5 0.0 copy-start.4
  159.5 0.0 copy-start.6
  159.5 1.2 copy.41
  160.7 0.0 copy-done.5
  160.7 0.7 copy.42
  161.4 0.0 copy-done.4
  161.4 0.7 copy.43
  162.1 0.0 copy-done.6
  162.1 0.6 copy.44
  (1 shorter events, 0.0 us)
Async XLA Ops:
  150.3 5.2 %copy-start.3 = (bf16[256,1792]{1,0:T(8,128)(2,1)S(1)}, bf16[256,1792]{1,0:T(8,128)(2,1)}, u32[]{:S(2)}) copy-start(bf16[256,1792]{1,0:T(8,128)(2,1)} %get-tuple-element.60) | copy-start | bytes 2752516
  153.2 3.2 %copy-start.2 = (bf16[256,1792]{1,0:T(8,128)(2,1)S(1)}, bf16[256,1792]{1,0:T(8,128)(2,1)}, u32[]{:S(2)}) copy-start(bf16[256,1792]{1,0:T(8,128)(2,1)} %get-tuple-element.61) | copy-start | bytes 2752516
  155.5 1.9 %copy-start.1 = (bf16[256,3584]{1,0:T(8,128)(2,1)S(1)}, bf16[256,3584]{1,0:T(8,128)(2,1)}, u32[]{:S(2)}) copy-start(bf16[256,3584]{1,0:T(8,128)(2,1)} %get-tuple-element.62) | copy-start | bytes 5505028
  157.3 2.2 %copy-start = (bf16[256,3584]{1,0:T(8,128)(2,1)S(1)}, bf16[256,3584]{1,0:T(8,128)(2,1)}, u32[]{:S(2)}) copy-start(bf16[256,3584]{1,0:T(8,128)(2,1)} %get-tuple-element.63) | copy-start | bytes 5505028
  159.5 1.2 copy-start.5
  159.5 1.9 %copy-start.4 = (f32[256,128]{1,0:T(8,128)S(1)}, f32[256,128]{1,0:T(8,128)}, u32[]{:S(2)}) copy-start(f32[256,128]{1,0:T(8,128)} %get-tuple-element.66) | copy-start | bytes 393220
  159.5 2.5 %copy-start.6 = (f32[4,3584]{1,0:T(4,128)S(1)}, f32[4,3584]{1,0:T(4,128)}, u32[]{:S(2)}) copy-start(f32[4,3584]{1,0:T(4,128)} %get-tuple-element.67) | copy-start | bytes 172036
where the time goes:
time: 163 us
  Pallas kernels  147 us (90%)
  local copies, waits for them, and re-layouts  14.5 us (9%)
    pallas_call x1, Pallas kernels, local(): pl.pallas_call(functools.partial(kernel, sizes), in_specs=[vmem] * len(in...  147 us
    unnamed x24, local copies, waits for them, and re-layouts  12.6 us

commit v1 on v0

--- a/solution.py
+++ b/solution.py
@@ -217,21 +217,26 @@
             r.kv[hh, a, aligned(span + place * R, R), :] = r.send[mine, a]
             r.qd[hh, a, aligned(place * R, R), :] = r.send[mine, 2 + a]
 
-    for h in range(H):
+    def pack_all(hh):
         for a, ref in enumerate((r.k, r.v, r.q, r.do)):
-            pack(ref, h, a)
-    for hh in range(per):
+            for p in range(G):
+                pack(ref, per * p + hh, a)
+
+    def send_all(hh):
         for d in others:
             kv_out(hh, d).start()
         for d in others:
             qd_out(hh, d).start()
-    for hh in range(per):
         own_piece(hh)
 
-    @pl.when(has_next)
-    def _():
-        for hh in range(per):
+        @pl.when(has_next)
+        def _():
             forward(hh, 0).start()
+
+    pack_all(0)
+    send_all(0)
+    for hh in range(1, per):
+        pack_all(hh)
 
     @pl.when(jnp.logical_not(has_prev))
     def _():
@@ -341,8 +346,10 @@
         if c > 0:
             pass_on(0, c)
     state, decay = Exchange(state_out, others), Exchange(decay_out, others)
+    decay.start()
     state.start()
-    decay.start()
+    for hh in range(1, per):
+        send_all(hh)
     r.st_a[place] = r.st_s[place]
     r.th_a[place] = r.th_s[place]
 
@@ -698,12 +705,11 @@
         spill = jnp.concatenate([jnp.zeros((EDGE - PAD, C), F32), r.spill[...]], axis=0)
         r.gconv[R - EDGE :, :] = (r.keep[...] + spill).astype(BF16)
 
-    def unpack():
+    def unpack(arrays, arriving):
         for hh in range(per):
             for d in others:
-                dq_out(hh, d).wait_recv()
-                dkv_out(hh, d).wait_recv()
-        for a, ref in enumerate((r.gq, r.gk, r.gv)):
+                arriving(hh, d).wait_recv()
+        for a, ref in arrays:
             open_tile = None
             for h in range(H):
                 first, last, off = window(h, ref)
@@ -720,27 +726,28 @@
                     ref[:, first + n * LANES : first + (n + 1) * LANES] = tile.astype(BF16)
                 open_tile = tiles[-1]
 
-    for hh in range(1, per):
-        for d in others:
-            pass_on(hh, d)
     attention_inputs(0)
     attention(0)
     chain_out()
     for hh in range(1, per):
+        for d in others:
+            pass_on(hh, d)
+    chain_in()
+    for hh in range(1, per):
         attention_inputs(hh)
         attention(hh)
-    chain_in()
+    for hh in range(per - 1):
+        give_back(hh)
     mixer_start()
     for c in range(G):
+        if c == G - 1:
+            unpack(((0, r.gq),), dq_out)
+            give_back(per - 1)
         mixer(c)
-        if c < per:
-            give_back(c)
-    for hh in range(G, per):
-        give_back(hh)
     mixer_end()
     sums_planes()
-    unpack()
     sums_all()
+    unpack(((1, r.gk), (2, r.gv)), dkv_out)
     sums_end()
 
     for hh in range(per):
@@ -790,6 +797,34 @@
     @pl.when(index > 0)
     def _():
         spill_out().wait_send()
+
+
+def copy_kernel(*refs):
+    for source, target in zip(refs[: len(refs) // 2], refs[len(refs) // 2 :]):
+        target[...] = source[...]
+
+
+def written(arrays, steps=7):
+    large = lambda a: a.shape[1] % (steps * LANES) == 0 and a.dtype == BF16
+    spec = lambda a: (
+        pl.BlockSpec((a.shape[0], a.shape[1] // steps), lambda n: (0, n))
+        if large(a) else pl.BlockSpec(a.shape, lambda n: (0, 0))
+    )
+    specs = [spec(a) for a in arrays]
+    return pl.pallas_call(
+        copy_kernel,
+        grid=(steps,),
+        in_specs=specs,
+        out_specs=specs,
+        out_shape=[jax.ShapeDtypeStruct(a.shape, a.dtype) for a in arrays],
+        name="written",
+        compiler_params=pltpu.CompilerParams(
+            dimension_semantics=("arbitrary",), vmem_limit_bytes=67_043_328
+        ),
+        cost_estimate=pl.CostEstimate(
+            flops=2_000_000_000, bytes_accessed=14_000_000, transcendentals=0
+        ),
+    )(*arrays)
 
 
 def local(
@@ -874,7 +909,7 @@
         head_count=head_count, names=[*inputs, *outputs, *scratch],
     )
     vmem = pl.BlockSpec(memory_space=pltpu.VMEM)
-    gq, gk, gv, gconv, ggate, gstep, gb, gc, gcw, small = pl.pallas_call(
+    found = pl.pallas_call(
         functools.partial(kernel, sizes),
         in_specs=[vmem] * len(inputs),
         out_specs=[vmem] * len(outputs),
@@ -888,6 +923,7 @@
             flops=60_000_000_000, bytes_accessed=20_000_000, transcendentals=0
         ),
     )(*inputs.values())
+    gq, gk, gv, gconv, ggate, gstep, gb, gc, gcw, small = written(found)
     bias, rate, skip = (small[KERNEL + n, :ssm_heads] for n in range(3))
     return gq, gk, gv, gconv, ggate, gstep, gb, gc, gcw, bias, rate, skip
 

time: 163 us -> 155 us (0.951)
  local copies, waits for them, and re-layouts: 14.5 us -> 5.12 us
    unnamed x24 -> x2, local copies, waits for them, and re-layouts: 12.6 us -> 3.18 us
    pallas_call x0 -> x1, Pallas kernels: none -> 8.27 us  [written(): pl.pallas_call(copy_kernel, grid=(steps,), in_specs=specs, out_specs=spec...]
    pallas_call x1, Pallas kernels: 147 us -> 140 us  [local(): pl.pallas_call(functools.partial(kernel, sizes), in_specs=[vmem] * len(in...]
where the time goes in v1:
time: 155 us
  Pallas kernels  148 us (95%)
  local copies, waits for them, and re-layouts  5.12 us (3%)
    pallas_call x1, Pallas kernels, local(): pl.pallas_call(functools.partial(kernel, sizes), in_specs=[vmem] * len(in...  140 us
    pallas_call x1, Pallas kernels, written(): pl.pallas_call(copy_kernel, grid=(steps,), in_specs=specs, out_specs=spec...  8.27 us
    unnamed x2, local copies, waits for them, and re-layouts  3.18 us

profile of v1, /device:TPU:0, one launch (start us, length us, event | category | flops | bytes accessed | tf_op | source)
XLA Modules:
  0.0 155.0 jit_solution(10254992702655927776)
XLA Ops:
  0.6 0.7 convert_element_type.3
  1.4 0.6 reshape.27.refs_4_
  2.0 1.6 %copy.27.refs_9_ = f32[256,56]{1,0:T(8,128)} copy(f32[256,56]{0,1:T(8,128)} %param.22) | data formatting | bytes 114688 | tf_op args[7]
  3.6 140.2 %pair.1 = (bf16[256,1792]{1,0:T(8,128)(2,1)}, bf16[256,1792]{1,0:T(8,128)(2,1)}, bf16[256,1792]{1,0:T(8,128)(2,1)}, bf16[256,3584]{1,0:T(8,128)(2,1)}, bf16[256,...) custom-call(bf16[256,1792]{1,0:T(8,128)(2,1)} %refs_0_.1, ...), custom_call_target="tpu_custom_call" | custom-call | flops 60000002048 | bytes 20000000 | tf_op jit(solution)/shard_map/pair/pallas_call | solution.py:912
  143.8 8.3 %written.1 = (bf16[256,1792]{1,0:T(8,128)(2,1)}, bf16[256,1792]{1,0:T(8,128)(2,1)}, bf16[256,1792]{1,0:T(8,128)(2,1)}, bf16[256,3584]{1,0:T(8,128)(2,1)}, bf16[2...) custom-call(bf16[256,1792]{1,0:T(8,128)(2,1)} %get-tuple-element.32., ...), custom_call_target="tpu_custom_call" | custom-call | flops 2000000000 | bytes 14000000 | tf_op jit(solution)/shard_map/written/pallas_call | solution.py:814
  152.1 1.3 slice_bitcast_fusion
  153.4 1.6 %copy.28 = f32[256,56]{0,1:T(8,128)} copy(f32[256,56]{1,0:T(8,128)} %get-tuple-element.57) | data formatting | bytes 114688
  (1 shorter events, 0.0 us)
